TPU v7x, 32 devices: a whole 2x2x4 slice. The times are simulated.
32 devices in a mesh: row: 4 (over y, x), col: 8 (over z, core).
Axes of the slice: x: 2, y: 2, z: 4, core: 2. Of those that a mesh axis runs over, the one named last changes fastest.
Arguments:
- tile_weights: bfloat16 [4, 8, 2, 128, 128], P('row', 'col'), may hold values from 0 to 4, as said below
- tile_pos: int32 [4, 8, 2, 2], P('row', 'col'), may hold values from 0 to 1, as said below
- tile_total: int32 [4, 8], P('row', 'col'), may hold values from 1 to 2, as said below
- root_ids: int32 [128], replicated, may hold values from 0 to 1023
Outputs:
- hop_level: int32 [1024, 128], P(('row', 'col'))
- path_share: float32 [1024, 128], P(('row', 'col'))
- found_per_level: float32 [4, 128], replicated
Inputs may be any that keep to these rules, and one draw needn't show every extreme that they name: `tile_weights`: nonnegative; an entry is zero wherever the tile has no edge. `tile_pos`: the slots of one device name distinct tile positions; tile rows lie below 2 and tile columns below 1. `tile_total`: some device uses all 2 slots; slots at or past a device's total hold arbitrary positions and zero weights.
All inputs are finite; a program needn't handle non-finite values.
Results may differ from a plain program's by a relative error of at most 0.01.
Values may be sent and summed in bfloat16 or wider, within the bound.
A program may use at most 64 MiB of HBM per device.

v0:
```python
import jax
import jax.numpy as jnp
from jax import lax
from jax.sharding import PartitionSpec as P

ROOTS = 128
PV = 32
LEVELS = 4


def tile_products(source_rows, live_tiles, dest_slots, source_slots, row_tiles):
    source_tiles = source_rows.reshape(-1, 128, source_rows.shape[1])
    blocks = source_tiles[source_slots]
    products = jnp.einsum("src,sck->srk", live_tiles, blocks, preferred_element_type=jnp.float32)
    partial_value = jnp.zeros((row_tiles, 128, source_rows.shape[1]), jnp.float32)
    partial_value = partial_value.at[dest_slots].add(products)
    return partial_value.reshape(row_tiles * 128, source_rows.shape[1])


def local(tile_weights, tile_pos, tile_total, root_ids):
    col_devices = lax.axis_size("col")
    row_index = lax.axis_index("row")
    col_index = lax.axis_index("col")
    tile_data = tile_weights[0, 0]
    positions = tile_pos[0, 0]
    slot_limit = tile_total[0, 0]
    slot_total = tile_data.shape[0]
    in_use = (jnp.arange(slot_total, dtype=jnp.int32) < slot_limit).astype(jnp.bfloat16)
    live_tiles = tile_data * in_use[:, None, None]
    dest_slots = positions[0]
    source_slots = positions[1]
    row_block = col_devices * PV
    row_tiles = row_block // 128
    state_start = (row_index * col_devices + col_index) * PV
    state_rows = PV
    vertex_ids = state_start + jnp.arange(state_rows, dtype=jnp.int32)
    is_root = vertex_ids[:, None] == root_ids[None, :]
    kept_weight = is_root.astype(jnp.float32)
    path_now = is_root.astype(jnp.bfloat16)
    hop_level = jnp.where(is_root, 0, LEVELS + 1).astype(jnp.int32)
    found_counts = []
    found_totals = []
    for level_num in range(LEVELS):
        own_front = path_now
        source_rows = lax.all_gather(own_front, "row", axis=0, tiled=True)
        partial_value = tile_products(source_rows, live_tiles, dest_slots, source_slots, row_tiles)
        arrived = lax.psum_scatter(
            partial_value.astype(jnp.bfloat16), "col", scatter_dimension=0, tiled=True
        ).astype(jnp.float32)
        newly = (arrived > 0) & (hop_level == LEVELS + 1)
        path_weight = jnp.where(newly, arrived, jnp.float32(0.0))
        hop_level = jnp.where(newly, jnp.int32(level_num + 1), hop_level)
        kept_weight = kept_weight + path_weight
        path_now = path_weight.astype(jnp.bfloat16)
        found_count = jnp.sum(newly.astype(jnp.float32), axis=0)
        found_total = jnp.sum(path_weight, axis=0)
        found_counts.append(found_count)
        found_totals.append(found_total)
    counts = jnp.stack(found_counts)
    totals = jnp.stack(found_totals)
    counts, totals = lax.psum((counts, totals), ("row", "col"))
    factor = counts / jnp.maximum(totals, 1.0)
    factor_table = jnp.concatenate(
        [jnp.ones((1, ROOTS), jnp.float32), factor, jnp.zeros((1, ROOTS), jnp.float32)], axis=0
    )
    scale = jnp.zeros_like(kept_weight)
    for level_num in range(LEVELS + 2):
        scale = scale + jnp.where(
            hop_level == level_num, factor_table[level_num][None, :], jnp.float32(0.0)
        )
    return (hop_level, kept_weight * scale, counts)


def solution(mesh):
    placed = (P("row", "col", None, None, None), P("row", "col", None, None), P("row", "col"), P())
    return jax.shard_map(
        local,
        mesh=mesh,
        in_specs=placed,
        out_specs=(P(("row", "col"), None), P(("row", "col"), None), P()),
        check_vma=False,
    )
```

profile of v0, /device:TPU:1, one launch (start us, length us, event | category | flops | bytes accessed | tf_op | source)
XLA Modules:
  0.0 212.5 jit_solution(12147868327278820978)
XLA Ops:
  7.9 0.7 fusion.35
  8.6 0.7 compare_convert_fusion.1
  9.3 7.0 %all_gather.12 = bf16[128,128]{1,0:T(8,128)(2,1)S(1)} all-gather(bf16[32,128]{1,0:T(8,128)(2,1)S(1)} %compare_convert_fusion.1), channel_id=1, replica_groups=mesh['row'=4,'col'=8] {'row'}, dimensions={0}, use_global_device_ids=true | all-gather | bytes 40960 | tf_op jit(solution)/shard_map/all_gather | solution.py:45
  16.5 0.6 scatter_fusion
  17.2 0.6 convert_element_type.72
  17.9 29.6 %reduce-scatter.5.cloned.1.call-done = bf16[32,128]{1,0:T(8,128)(2,1)} async-done(((bf16[256,128]{1,0:T(8,128)(2,1)}), bf16[32,128]{1,0:T(8,128)(2,1)}) %reduce-scatter.5.cloned.1.call-update) | async-done | bytes 8208 | tf_op jit(solution)/shard_map/reduce_scatter | solution.py:47
  47.4 0.9 fusion.16
  48.3 6.5 %all_gather.13 = bf16[128,128]{1,0:T(8,128)(2,1)S(1)} all-gather(bf16[32,128]{1,0:T(8,128)(2,1)S(1)} %fusion.18), channel_id=1, replica_groups=mesh['row'=4,'col'=8] {'row'}, dimensions={0}, use_global_device_ids=true | all-gather | bytes 40960 | tf_op jit(solution)/shard_map/all_gather | solution.py:45
  55.0 0.6 scatter_fusion.1
  55.7 0.6 convert_element_type.76
  56.4 29.5 %reduce-scatter.7.cloned.1.call-done = bf16[32,128]{1,0:T(8,128)(2,1)} async-done(((bf16[256,128]{1,0:T(8,128)(2,1)}), bf16[32,128]{1,0:T(8,128)(2,1)}) %reduce-scatter.7.cloned.1.call-update) | async-done | bytes 8208 | tf_op jit(solution)/shard_map/reduce_scatter | solution.py:47
  85.9 0.9 fusion.19
  86.8 6.5 %all_gather.14 = bf16[128,128]{1,0:T(8,128)(2,1)S(1)} all-gather(bf16[32,128]{1,0:T(8,128)(2,1)S(1)} %fusion.21), channel_id=1, replica_groups=mesh['row'=4,'col'=8] {'row'}, dimensions={0}, use_global_device_ids=true | all-gather | bytes 40960 | tf_op jit(solution)/shard_map/all_gather | solution.py:45
  93.5 0.6 scatter_fusion.2
  94.2 0.6 convert_element_type.80
  94.9 29.5 %reduce-scatter.9.cloned.1.call-done = bf16[32,128]{1,0:T(8,128)(2,1)} async-done(((bf16[256,128]{1,0:T(8,128)(2,1)}), bf16[32,128]{1,0:T(8,128)(2,1)}) %reduce-scatter.9.cloned.1.call-update) | async-done | bytes 8208 | tf_op jit(solution)/shard_map/reduce_scatter | solution.py:47
  124.4 0.9 fusion.22
  125.2 6.5 %all_gather.15 = bf16[128,128]{1,0:T(8,128)(2,1)S(1)} all-gather(bf16[32,128]{1,0:T(8,128)(2,1)S(1)} %fusion.24), channel_id=1, replica_groups=mesh['row'=4,'col'=8] {'row'}, dimensions={0}, use_global_device_ids=true | all-gather | bytes 40960 | tf_op jit(solution)/shard_map/all_gather | solution.py:45
  132.0 0.6 scatter_fusion.3
  133.3 29.6 %reduce-scatter.11.cloned.1.call-done = bf16[32,128]{1,0:T(8,128)(2,1)} async-done(((bf16[256,128]{1,0:T(8,128)(2,1)}), bf16[32,128]{1,0:T(8,128)(2,1)}) %reduce-scatter.11.cloned.1.call-update) | async-done | bytes 8208 | tf_op jit(solution)/shard_map/reduce_scatter | solution.py:47
  162.8 0.8 fusion.25
  163.6 40.4 %all-reduce = (f32[4,128]{1,0:T(4,128)S(1)}, f32[4,128]{1,0:T(4,128)S(1)}) all-reduce(f32[4,128]{1,0:T(4,128)S(1)} %get-tuple-element.23, f32[4,128]{1,0:T(4,128)S(1)} %get-tuple-element.24), channel_id=1, replica_groups=mesh['row'=4,'col'=8] {'row','col'}, use_global_device_ids=true, to_apply=%region_12.13 | all-reduce | flops 1024 | bytes 8192 | tf_op jit(solution)/shard_map/psum | solution.py:61
  204.6 0.7 copy-done.4
  205.3 0.7 fusion.29
  (38 shorter events, 2.4 us)
Async XLA Ops:
  7.2 9.1 %copy-start = (bf16[1,1,2,128,128]{4,3,2,1,0:T(8,128)(2,1)S(1)}, bf16[1,1,2,128,128]{4,3,2,1,0:T(8,128)(2,1)}, u32[]{:S(2)}) copy-start(bf16[1,1,2,128,128]{4,3,2,1,0:T(8,128)(2,1)} %param.4) | copy-start | bytes 196612
  7.2 40.3 %reduce-scatter.5.cloned.1.call-start = ((), (), s32[]{:S(2)}) async-start(), calls=%async_computation.4 | async-start | bytes 73728 | tf_op jit(solution)/shard_map/reduce_scatter | solution.py:47
  17.8 29.6 %copy-start.5 = (s32[128]{0:T(128)S(1)}, s32[128]{0:T(128)}, u32[]{:S(2)}) copy-start(s32[128]{0:T(128)} %param.7) | copy-start | bytes 1540
  17.8 68.1 %reduce-scatter.7.cloned.1.call-start = ((), (), s32[]{:S(2)}) async-start(), calls=%async_computation.5 | async-start | bytes 73728 | tf_op jit(solution)/shard_map/reduce_scatter | solution.py:47
  47.4 0.9 copy-start.1
  56.3 68.0 %reduce-scatter.9.cloned.1.call-start = ((), (), s32[]{:S(2)}) async-start(), calls=%async_computation.6 | async-start | bytes 73728 | tf_op jit(solution)/shard_map/reduce_scatter | solution.py:47
  85.9 0.9 copy-start.2
  94.8 68.0 %reduce-scatter.11.cloned.1.call-start = ((), (), s32[]{:S(2)}) async-start(), calls=%async_computation.7 | async-start | bytes 73728 | tf_op jit(solution)/shard_map/reduce_scatter | solution.py:47
  124.4 0.9 copy-start.3
  204.0 0.6 copy-start.6
  204.6 0.7 copy-start.4
Sparse Core Ops, SparseCore 0:
  17.9 29.4 reduce-scatter.4
  56.5 29.4 reduce-scatter.6
  95.0 29.3 reduce-scatter.8
  133.4 29.3 reduce-scatter.10
where the time goes:
time: 215 us; the launch traced here: 213 us
  waiting for transfers between devices  118 us (55%)
  blocking collectives  66.8 us (31%)
  between operations  14.6 us (7%)
  other arithmetic  10.6 us (5%)
    reduce_scatter x4, waiting for transfers between devices, local(): lax.psum_scatter(partial_value.astype(jnp.bfloat16), 'col', scatter_dimen...  118 us
    psum x1, blocking collectives, local(): counts, totals = lax.psum((counts, totals), ('row', 'col'))  40.4 us
    all_gather x4, blocking collectives, local(): source_rows = lax.all_gather(own_front, 'row', axis=0, tiled=True)  26.4 us
  transfers between devices with their start and end apart: 4, of which 4 were waited for; matrix products, arithmetic and copies ran while one was open for 0% of the time, Pallas kernels for 0%

commit v1 on v0

--- a/solution.py
+++ b/solution.py
@@ -1,11 +1,17 @@
+import functools
+
 import jax
 import jax.numpy as jnp
 from jax import lax
+from jax.experimental import pallas as pl
+from jax.experimental.pallas import tpu as pltpu
 from jax.sharding import PartitionSpec as P
 
 ROOTS = 128
 PV = 32
 LEVELS = 4
+TILE = 128
+REPLICA_LIMIT = 16 * 2**20
 
 
 def tile_products(source_rows, live_tiles, dest_slots, source_slots, row_tiles):
@@ -71,10 +77,212 @@
     return (hop_level, kept_weight * scale, counts)
 
 
+def near_order(depth):
+    table = []
+    for z in range(depth):
+        up = z < depth / 2
+        others = [other for other in range(depth) if other != z]
+        table.append(sorted(others, key=lambda o: (abs(o - z), (o < z) if up else (o > z))))
+    return table
+
+
+def pick(table, z, step):
+    value = jnp.int32(0)
+    for index, entries in enumerate(table):
+        value = jnp.where(z == index, jnp.int32(entries[step]), value)
+    return value
+
+
+def kernel(
+    n_row, n_col, tiles_ref, pos_ref, total_ref, roots_ref, hop_out, share_out, counts_out,
+    adj, front, hop, path, send_z, recv_z, send_n, recv_n, send_d, recv_d, send_s, recv_s, recv_sd,
+):
+    r = lax.axis_index("row")
+    c = lax.axis_index("col")
+    z, core = c // 2, c % 2
+    y, x = r // 2, r % 2
+    row_x, row_y, row_d = y * 2 + (1 - x), (1 - y) * 2 + x, (1 - y) * 2 + (1 - x)
+    rows = (row_x, row_y)
+    depth = n_col // 2
+    slots = tiles_ref.shape[0]
+    row_block, col_block = adj.shape[2], adj.shape[3]
+    half = row_block // 2
+    roots = roots_ref.shape[1]
+    table = near_order(depth)
+
+    barrier = pltpu.get_barrier_semaphore()
+    others = [(r, pick(table, z, step) * 2 + core) for step in range(depth - 1)]
+    others += [(row_x, c), (row_y, c), (r, z * 2 + 1 - core)]
+    for device in others:
+        pl.semaphore_signal(barrier, inc=1, device_id=device, device_id_type=pl.DeviceIdType.MESH)
+
+    for tr in range(row_block // TILE):
+        for tc in range(col_block // TILE):
+            value = jnp.zeros((TILE, TILE), jnp.float32)
+            for s in range(slots):
+                here = (pos_ref[0, s] == tr) & (pos_ref[1, s] == tc) & (s < total_ref[0, 0])
+                value = value + tiles_ref[s].astype(jnp.float32) * here.astype(jnp.float32)
+            adj[c, r, pl.ds(tr * TILE, TILE), pl.ds(tc * TILE, TILE)] = value.astype(jnp.bfloat16)
+
+    for rr in range(n_row):
+        part = pl.ds(rr * row_block, row_block)
+        ids = rr * row_block + lax.broadcasted_iota(jnp.int32, (row_block, roots), 0)
+        is_root = ids == roots_ref[...]
+        hop[part] = jnp.where(is_root, 0, LEVELS + 1).astype(jnp.int32)
+        path[part] = is_root.astype(jnp.float32)
+        for cc in range(n_col):
+            front[0, pl.ds(cc * col_block + rr * PV, PV)] = (
+                is_root[cc * PV:(cc + 1) * PV].astype(jnp.float32).astype(jnp.bfloat16)
+            )
+
+    pl.semaphore_wait(barrier, len(others))
+
+    started = []
+
+    def send(ref, send_sem, recv_sem, device):
+        copy = pltpu.make_async_remote_copy(
+            src_ref=ref, dst_ref=ref, send_sem=send_sem, recv_sem=recv_sem,
+            device_id=device, device_id_type=pl.DeviceIdType.MESH,
+        )
+        copy.start()
+        started.append(copy)
+
+    def arrive(ref, send_sem, recv_sem):
+        pltpu.make_async_remote_copy(
+            src_ref=ref, dst_ref=ref, send_sem=send_sem, recv_sem=recv_sem,
+            device_id=(r, z * 2 + 1 - core), device_id_type=pl.DeviceIdType.MESH,
+        ).wait_recv()
+
+    def block(zz, rr):
+        return adj.at[zz * 2 + core, rr]
+
+    def piece(zz, rr, h):
+        return adj.at[zz * 2 + core, rr, pl.ds(h * half, half)]
+
+    sibling = (r, z * 2 + 1 - core)
+
+    def spread(zz):
+        for axis in range(2):
+            send(block(zz, r), send_n.at[axis, zz], recv_n.at[axis, zz], (rows[axis], c))
+
+    def share_block(zz, rr):
+        send(block(zz, rr), send_s.at[rr, zz], recv_s.at[rr, zz], sibling)
+
+    def relay(zz):
+        for axis in range(2):
+            arrive(block(zz, rows[axis]), send_n.at[axis, zz], recv_n.at[axis, zz])
+            send(piece(zz, rows[axis], axis), send_d.at[axis, zz], recv_d.at[axis, zz], (rows[1 - axis], c))
+        for axis in range(2):
+            share_block(zz, rows[axis])
+
+    def finish(zz):
+        for axis in range(2):
+            arrive(piece(zz, row_d, axis), send_d.at[axis, zz], recv_d.at[axis, zz])
+            send(piece(zz, row_d, axis), send_s.at[n_row + axis, zz], recv_sd.at[axis, zz], sibling)
+
+    order = [z] + [pick(table, z, step) for step in range(depth - 1)]
+    spread(z)
+    for step in range(depth - 1):
+        zz = order[step + 1]
+        send(block(z, r), send_z.at[zz], recv_z.at[z], (r, zz * 2 + core))
+    share_block(z, r)
+    for step in range(depth):
+        if step + 1 < depth:
+            zz = order[step + 1]
+            arrive(block(zz, r), send_z.at[zz], recv_z.at[zz])
+            spread(zz)
+            share_block(zz, r)
+        relay(order[step])
+        if step > 0:
+            finish(order[step - 1])
+    finish(order[depth - 1])
+    for step in range(depth):
+        zz = order[step]
+        for rr in (r, row_x, row_y):
+            arrive(adj.at[zz * 2 + 1 - core, rr], send_s.at[rr, zz], recv_s.at[rr, zz])
+        for axis in range(2):
+            arrive(
+                adj.at[zz * 2 + 1 - core, row_d, pl.ds(axis * half, half)],
+                send_s.at[n_row + axis, zz], recv_sd.at[axis, zz],
+            )
+
+    own = pl.ds(pl.multiple_of((r * n_col + c) * PV, PV), PV)
+    kept = path[own]
+    factors = []
+    for level in range(LEVELS):
+        now, later = level % 2, (level + 1) % 2
+        count = jnp.zeros((1, roots), jnp.float32)
+        total = jnp.zeros((1, roots), jnp.float32)
+        source = front[now]
+        for rr in range(n_row):
+            part = pl.ds(rr * row_block, row_block)
+            wide = jnp.concatenate([adj[cc, rr] for cc in range(n_col)], axis=1)
+            arrived = jnp.dot(wide, source, preferred_element_type=jnp.float32)
+            old = hop[part]
+            newly = (arrived > 0) & (old == LEVELS + 1)
+            weight = jnp.where(newly, arrived, 0.0)
+            hop[part] = jnp.where(newly, level + 1, old)
+            path[part] = weight
+            count = count + jnp.sum(newly.astype(jnp.float32), axis=0, keepdims=True)
+            total = total + jnp.sum(weight, axis=0, keepdims=True)
+            narrow = weight.astype(jnp.bfloat16)
+            if level + 1 < LEVELS:
+                for cc in range(n_col):
+                    front[later, pl.ds(cc * col_block + rr * PV, PV)] = narrow[cc * PV:(cc + 1) * PV]
+        kept = kept + path[own]
+        counts_out[pl.ds(level, 1)] = count
+        factors.append(count / jnp.maximum(total, 1.0))
+    level_own = hop[own]
+    scale = jnp.where(level_own == 0, 1.0, 0.0)
+    for level in range(LEVELS):
+        scale = jnp.where(level_own == level + 1, factors[level], scale)
+    hop_out[...] = level_own
+    share_out[...] = kept * scale
+
+    for copy in started:
+        copy.wait_send()
+
+
+def replicated(n_row, n_col, tile_weights, tile_pos, tile_total, root_ids):
+    roots = root_ids.shape[0]
+    row_block, col_block = n_col * PV, n_row * PV
+    vertices = n_row * row_block
+    depth = n_col // 2
+    vmem = pl.BlockSpec(memory_space=pltpu.VMEM)
+    smem = pl.BlockSpec(memory_space=pltpu.SMEM)
+    dma = pltpu.SemaphoreType.DMA
+    return pl.pallas_call(
+        functools.partial(kernel, n_row, n_col),
+        out_shape=(
+            jax.ShapeDtypeStruct((PV, roots), jnp.int32),
+            jax.ShapeDtypeStruct((PV, roots), jnp.float32),
+            jax.ShapeDtypeStruct((LEVELS, roots), jnp.float32),
+        ),
+        in_specs=[vmem, smem, smem, vmem],
+        out_specs=(vmem, vmem, vmem),
+        scratch_shapes=[
+            pltpu.VMEM((n_col, n_row, row_block, col_block), jnp.bfloat16),
+            pltpu.VMEM((2, vertices, roots), jnp.bfloat16),
+            pltpu.VMEM((vertices, roots), jnp.int32),
+            pltpu.VMEM((vertices, roots), jnp.float32),
+            dma((depth,)), dma((depth,)),
+            dma((2, depth)), dma((2, depth)),
+            dma((2, depth)), dma((2, depth)),
+            dma((n_row + 2, depth)), dma((n_row, depth)), dma((2, depth)),
+        ],
+        compiler_params=pltpu.CompilerParams(collective_id=0, has_side_effects=True),
+    )(tile_weights[0, 0], tile_pos[0, 0], tile_total, root_ids.reshape(1, roots))
+
+
 def solution(mesh):
+    n_row, n_col = mesh.shape["row"], mesh.shape["col"]
+    vertices = n_row * n_col * PV
     placed = (P("row", "col", None, None, None), P("row", "col", None, None), P("row", "col"), P())
+    body = local
+    if n_row == 4 and n_col % 2 == 0 and 2 * vertices * vertices <= REPLICA_LIMIT:
+        body = functools.partial(replicated, n_row, n_col)
     return jax.shard_map(
-        local,
+        body,
         mesh=mesh,
         in_specs=placed,
         out_specs=(P(("row", "col"), None), P(("row", "col"), None), P()),

time: 215 us -> 30 us (0.14); the launches traced: 213 us -> 29.7 us
  waiting for transfers between devices: 118 us -> 0 us
  blocking collectives: 66.8 us -> 0 us
  Pallas kernels: 0 us -> 25.8 us
  between operations: 14.6 us -> 1.3 us
  other arithmetic: 10.6 us -> 0 us
    reduce_scatter x4 -> x0, waiting for transfers between devices: 118 us -> none  [local(): lax.psum_scatter(partial_value.astype(jnp.bfloat16), 'col', scatter_dimen...]
    psum x1 -> x0, blocking collectives: 40.4 us -> none  [local(): counts, totals = lax.psum((counts, totals), ('row', 'col'))]
    all_gather x4 -> x0, blocking collectives: 26.4 us -> none  [local(): source_rows = lax.all_gather(own_front, 'row', axis=0, tiled=True)]
    pallas_call x0 -> x1, Pallas kernels: none -> 25.8 us  [replicated(): pl.pallas_call(functools.partial(kernel, n_row, n_col), out_shape=(jax.Sh...]
    reduce_sum x4 -> x0, other arithmetic: 3.36 us -> none  [local(): found_total = jnp.sum(path_weight, axis=0)]
    convert_element_type x9 -> x0, other arithmetic: 3.27 us -> none  [the longest x4 2.52 us: local(): partial_value.astype(jnp.bfloat16)]
    scatter-add x4 -> x0, other arithmetic: 2.56 us -> none  [tile_products(): partial_value = partial_value.at[dest_slots].add(products)]
  transfers between devices with their start and end apart: 4 -> 0, of which waited for: 4 -> 0; matrix products, arithmetic and copies ran while one was open for 0% -> 0% of each run, Pallas kernels for 0% -> 0%
where the time goes in v1:
time: 30 us; the launch traced here: 29.7 us
  Pallas kernels  25.8 us (86%)
  local copies, waits for them, and re-layouts  2.58 us (9%)
  between operations  1.3 us (4%)
    pallas_call x1, Pallas kernels, replicated(): pl.pallas_call(functools.partial(kernel, n_row, n_col), out_shape=(jax.Sh...  25.8 us
    unnamed x7, local copies, waits for them, and re-layouts  2.58 us

profile of v1, /device:TPU:1, one launch (start us, length us, event | category | flops | bytes accessed | tf_op | source)
XLA Modules:
  0.0 29.7 jit_solution(16991909037226969481)
XLA Ops:
  1.3 25.8 %shard_map.67 = (s32[32,128]{1,0:T(8,128)}, f32[32,128]{1,0:T(8,128)}, f32[4,128]{1,0:T(4,128)}) custom-call(bf16[2,128,128]{2,1,0:T(8,128)(2,1)} %bitcast.3, s32[2,2]{1,0:T(2,128)} %bitcast.4, s32[1,1]{1,0:T(1,128)S(6)} %copy.10.total_ref, s32[1,128]{1,0:T(1,128)} %bitcast.5), custom_call_target="tpu_custom_call" | custom-call | tf_op jit(solution)/shard_map/pallas_call | solution.py:254
  27.1 0.0 copy-start
  27.1 1.3 %copy.11 = s32[32,128]{1,0:T(8,128)} copy(s32[32,128]{1,0:T(8,128)} %get-tuple-element.6) | data formatting | bytes 32768
  28.5 0.0 copy-done
  28.5 0.0 copy-start.1
  28.5 0.6 %copy.12 = f32[32,128]{1,0:T(8,128)} copy(f32[32,128]{1,0:T(8,128)S(1)} %copy-done) | data formatting | bytes 32768
  29.1 0.1 copy-done.1
  29.1 0.6 %copy.13 = f32[4,128]{1,0:T(4,128)} copy(f32[4,128]{1,0:T(4,128)S(1)} %copy-done.1) | data formatting | bytes 4096
Async XLA Ops:
  27.1 1.3 %copy-start = (f32[32,128]{1,0:T(8,128)S(1)}, f32[32,128]{1,0:T(8,128)}, u32[]{:S(2)}) copy-start(f32[32,128]{1,0:T(8,128)} %get-tuple-element.7) | copy-start | bytes 49156
  28.5 0.7 %copy-start.1 = (f32[4,128]{1,0:T(4,128)S(1)}, f32[4,128]{1,0:T(4,128)}, u32[]{:S(2)}) copy-start(f32[4,128]{1,0:T(4,128)} %get-tuple-element.8) | copy-start | bytes 6148

commit v2 on v1

--- a/solution.py
+++ b/solution.py
@@ -12,6 +12,8 @@
 LEVELS = 4
 TILE = 128
 REPLICA_LIMIT = 16 * 2**20
+LATE = 4
+SENDS = 256
 
 
 def tile_products(source_rows, live_tiles, dest_slots, source_slots, row_tiles):
@@ -77,13 +79,16 @@
     return (hop_level, kept_weight * scale, counts)
 
 
-def near_order(depth):
-    table = []
-    for z in range(depth):
-        up = z < depth / 2
-        others = [other for other in range(depth) if other != z]
-        table.append(sorted(others, key=lambda o: (abs(o - z), (o < z) if up else (o > z))))
-    return table
+def arrival_order(depth):
+    def key(z, other):
+        inner = 0 < other < depth - 1
+        gap = abs(other - z)
+        return (gap > 1 or not inner, inner, -gap)
+    return [sorted((o for o in range(depth) if o != z), key=lambda o: key(z, o)) for z in range(depth)]
+
+
+def far_order(depth):
+    return [sorted((o for o in range(depth) if o != z), key=lambda o: -abs(o - z)) for z in range(depth)]
 
 
 def pick(table, z, step):
@@ -95,7 +100,7 @@
 
 def kernel(
     n_row, n_col, tiles_ref, pos_ref, total_ref, roots_ref, hop_out, share_out, counts_out,
-    adj, front, hop, path, send_z, recv_z, send_n, recv_n, send_d, recv_d, send_s, recv_s, recv_sd,
+    adj, front, hop, path, send_sem, recv_sem,
 ):
     r = lax.axis_index("row")
     c = lax.axis_index("col")
@@ -106,12 +111,16 @@
     depth = n_col // 2
     slots = tiles_ref.shape[0]
     row_block, col_block = adj.shape[2], adj.shape[3]
-    half = row_block // 2
+    tail = row_block // LATE // 2
+    body = row_block // 2 - tail
+    pieces = [(0, body), (body, body), (2 * body, tail), (2 * body + tail, tail)]
     roots = roots_ref.shape[1]
-    table = near_order(depth)
+    order_table, far_table = arrival_order(depth), far_order(depth)
+    order = [z] + [pick(order_table, z, step) for step in range(depth - 1)]
+    far = [pick(far_table, z, step) for step in range(depth - 1)]
 
     barrier = pltpu.get_barrier_semaphore()
-    others = [(r, pick(table, z, step) * 2 + core) for step in range(depth - 1)]
+    others = [(r, far[step] * 2 + core) for step in range(depth - 1)]
     others += [(row_x, c), (row_y, c), (r, z * 2 + 1 - core)]
     for device in others:
         pl.semaphore_signal(barrier, inc=1, device_id=device, device_id_type=pl.DeviceIdType.MESH)
@@ -139,72 +148,113 @@
 
     started = []
 
-    def send(ref, send_sem, recv_sem, device):
+    def each(piece, rr, zz):
+        return adj.at[zz * 2 + core, rr, pl.ds(*pieces[piece])]
+
+    def send(piece, rr, zz, device, when=None):
         copy = pltpu.make_async_remote_copy(
-            src_ref=ref, dst_ref=ref, send_sem=send_sem, recv_sem=recv_sem,
+            src_ref=each(piece, rr, zz), dst_ref=each(piece, rr, zz),
+            send_sem=send_sem.at[len(started)], recv_sem=recv_sem.at[piece, rr, zz * 2 + core],
             device_id=device, device_id_type=pl.DeviceIdType.MESH,
         )
-        copy.start()
-        started.append(copy)
-
-    def arrive(ref, send_sem, recv_sem):
+        started.append((copy, when))
+        if when is None:
+            copy.start()
+        else:
+            pl.when(when)(copy.start)
+
+    def arrive(piece, rr, cc):
+        ref = adj.at[cc, rr, pl.ds(*pieces[piece])]
         pltpu.make_async_remote_copy(
-            src_ref=ref, dst_ref=ref, send_sem=send_sem, recv_sem=recv_sem,
-            device_id=(r, z * 2 + 1 - core), device_id_type=pl.DeviceIdType.MESH,
+            src_ref=ref, dst_ref=ref, send_sem=send_sem.at[0], recv_sem=recv_sem.at[piece, rr, cc],
+            device_id=sibling, device_id_type=pl.DeviceIdType.MESH,
         ).wait_recv()
 
-    def block(zz, rr):
-        return adj.at[zz * 2 + core, rr]
-
-    def piece(zz, rr, h):
-        return adj.at[zz * 2 + core, rr, pl.ds(h * half, half)]
+    def here(piece, rr, zz):
+        arrive(piece, rr, zz * 2 + core)
 
     sibling = (r, z * 2 + 1 - core)
+    is_end = (z == 0) | (z == depth - 1)
+
+    def column(piece, rr):
+        for step in range(depth - 1):
+            zz = far[step]
+            near = (zz == z + 1) | (zz == z - 1)
+            send(piece, rr, z, (r, zz * 2 + core), is_end | near)
+
+    def onward(piece, rr, zz):
+        nxt = jnp.where(zz < z, z + 1, z - 1)
+        inner = (zz > 0) & (zz < depth - 1) & (nxt >= 0) & (nxt < depth)
+        nxt = jnp.where(inner, nxt, jnp.where(z > 0, 0, 1))
+        send(piece, rr, zz, (r, nxt * 2 + core), inner)
 
     def spread(zz):
-        for axis in range(2):
-            send(block(zz, r), send_n.at[axis, zz], recv_n.at[axis, zz], (rows[axis], c))
-
-    def share_block(zz, rr):
-        send(block(zz, rr), send_s.at[rr, zz], recv_s.at[rr, zz], sibling)
-
-    def relay(zz):
-        for axis in range(2):
-            arrive(block(zz, rows[axis]), send_n.at[axis, zz], recv_n.at[axis, zz])
-            send(piece(zz, rows[axis], axis), send_d.at[axis, zz], recv_d.at[axis, zz], (rows[1 - axis], c))
-        for axis in range(2):
-            share_block(zz, rows[axis])
-
-    def finish(zz):
-        for axis in range(2):
-            arrive(piece(zz, row_d, axis), send_d.at[axis, zz], recv_d.at[axis, zz])
-            send(piece(zz, row_d, axis), send_s.at[n_row + axis, zz], recv_sd.at[axis, zz], sibling)
-
-    order = [z] + [pick(table, z, step) for step in range(depth - 1)]
+        for turn in range(2):
+            for axis in range(2):
+                piece = axis if turn == 0 else 1 - axis
+                send(piece, r, zz, (rows[axis], c))
+
+    def relay(base, zz):
+        for axis in range(2):
+            here(base + axis, rows[axis], zz)
+            send(base + axis, rows[axis], zz, (rows[1 - axis], c))
+        for axis in range(2):
+            send(base + axis, rows[axis], zz, sibling)
+        for axis in range(2):
+            here(base + 1 - axis, rows[axis], zz)
+            send(base + 1 - axis, rows[axis], zz, sibling)
+
+    def finish(base, zz):
+        for axis in range(2):
+            here(base + axis, row_d, zz)
+            send(base + axis, row_d, zz, sibling)
+
+    def late(zz):
+        for rr in (r, row_x, row_y, row_d):
+            for piece in (2, 3):
+                here(piece, rr, zz)
+                onward(piece, rr, zz)
+                send(piece, rr, zz, sibling)
+
+    def climb(zz):
+        for piece in (0, 1):
+            here(piece, r, zz)
+            onward(piece, r, zz)
+        spread(zz)
+        for piece in (0, 1):
+            send(piece, r, zz, sibling)
+
+    for turn in range(2):
+        for axis in range(2):
+            send(2 + (axis if turn == 0 else 1 - axis), r, z, (rows[axis], c))
     spread(z)
-    for step in range(depth - 1):
-        zz = order[step + 1]
-        send(block(z, r), send_z.at[zz], recv_z.at[z], (r, zz * 2 + core))
-    share_block(z, r)
-    for step in range(depth):
+    for piece in range(2):
+        column(piece, r)
+    for piece in range(4):
+        send(piece, r, z, sibling)
+    relay(2, z)
+    for piece in (2, 3):
+        for rr in (r, row_x, row_y):
+            column(piece, rr)
+    relay(0, z)
+    climb(order[1])
+    finish(2, z)
+    for piece in (2, 3):
+        column(piece, row_d)
+    finish(0, z)
+    for step in range(1, depth):
         if step + 1 < depth:
-            zz = order[step + 1]
-            arrive(block(zz, r), send_z.at[zz], recv_z.at[zz])
-            spread(zz)
-            share_block(zz, r)
-        relay(order[step])
-        if step > 0:
-            finish(order[step - 1])
-    finish(order[depth - 1])
-    for step in range(depth):
-        zz = order[step]
-        for rr in (r, row_x, row_y):
-            arrive(adj.at[zz * 2 + 1 - core, rr], send_s.at[rr, zz], recv_s.at[rr, zz])
-        for axis in range(2):
-            arrive(
-                adj.at[zz * 2 + 1 - core, row_d, pl.ds(axis * half, half)],
-                send_s.at[n_row + axis, zz], recv_sd.at[axis, zz],
-            )
+            climb(order[step + 1])
+        relay(0, order[step])
+        if step > 1:
+            finish(0, order[step - 1])
+            late(order[step - 1])
+    finish(0, order[depth - 1])
+    late(order[depth - 1])
+    for rr in (r, row_x, row_y, row_d):
+        for step in range(depth):
+            for piece in range(4):
+                arrive(piece, rr, order[step] * 2 + 1 - core)
 
     own = pl.ds(pl.multiple_of((r * n_col + c) * PV, PV), PV)
     kept = path[own]
@@ -239,8 +289,11 @@
     hop_out[...] = level_own
     share_out[...] = kept * scale
 
-    for copy in started:
-        copy.wait_send()
+    for copy, when in started:
+        if when is None:
+            copy.wait_send()
+        else:
+            pl.when(when)(copy.wait_send)
 
 
 def replicated(n_row, n_col, tile_weights, tile_pos, tile_total, root_ids):
@@ -265,10 +318,8 @@
             pltpu.VMEM((2, vertices, roots), jnp.bfloat16),
             pltpu.VMEM((vertices, roots), jnp.int32),
             pltpu.VMEM((vertices, roots), jnp.float32),
-            dma((depth,)), dma((depth,)),
-            dma((2, depth)), dma((2, depth)),
-            dma((2, depth)), dma((2, depth)),
-            dma((n_row + 2, depth)), dma((n_row, depth)), dma((2, depth)),
+            dma((SENDS,)),
+            dma((4, n_row, n_col)),
         ],
         compiler_params=pltpu.CompilerParams(collective_id=0, has_side_effects=True),
     )(tile_weights[0, 0], tile_pos[0, 0], tile_total, root_ids.reshape(1, roots))
@@ -279,7 +330,7 @@
     vertices = n_row * n_col * PV
     placed = (P("row", "col", None, None, None), P("row", "col", None, None), P("row", "col"), P())
     body = local
-    if n_row == 4 and n_col % 2 == 0 and 2 * vertices * vertices <= REPLICA_LIMIT:
+    if n_row == 4 and n_col % 8 == 0 and 2 * vertices * vertices <= REPLICA_LIMIT:
         body = functools.partial(replicated, n_row, n_col)
     return jax.shard_map(
         body,

time: 30 us -> 32.3 us (1.077)
  Pallas kernels: 25.8 us -> 28.1 us
    pallas_call x1, Pallas kernels: 25.8 us -> 28.1 us  [replicated(): pl.pallas_call(functools.partial(kernel, n_row, n_col), out_shape=(jax.Sh...]
where the time goes in v2:
time: 32.3 us; the launch traced here: 32 us
  Pallas kernels  28.1 us (87%)
  local copies, waits for them, and re-layouts  2.58 us (8%)
  between operations  1.3 us (4%)
    pallas_call x1, Pallas kernels, replicated(): pl.pallas_call(functools.partial(kernel, n_row, n_col), out_shape=(jax.Sh...  28.1 us
    unnamed x7, local copies, waits for them, and re-layouts  2.58 us

profile of v2, /device:TPU:1, one launch (start us, length us, event | category | flops | bytes accessed | tf_op | source)
XLA Modules:
  0.0 32.0 jit_solution(11768959628697843111)
XLA Ops:
  1.3 28.1 %shard_map.67 = (s32[32,128]{1,0:T(8,128)}, f32[32,128]{1,0:T(8,128)}, f32[4,128]{1,0:T(4,128)}) custom-call(bf16[2,128,128]{2,1,0:T(8,128)(2,1)} %bitcast.3, s32[2,2]{1,0:T(2,128)} %bitcast.4, s32[1,1]{1,0:T(1,128)S(6)} %copy.10.total_ref, s32[1,128]{1,0:T(1,128)} %bitcast.5), custom_call_target="tpu_custom_call" | custom-call | tf_op jit(solution)/shard_map/pallas_call | solution.py:307
  29.4 0.0 copy-start
  29.4 1.3 %copy.11 = s32[32,128]{1,0:T(8,128)} copy(s32[32,128]{1,0:T(8,128)} %get-tuple-element.6) | data formatting | bytes 32768
  30.7 0.0 copy-done
  30.7 0.0 copy-start.1
  30.7 0.6 %copy.12 = f32[32,128]{1,0:T(8,128)} copy(f32[32,128]{1,0:T(8,128)S(1)} %copy-done) | data formatting | bytes 32768
  31.4 0.1 copy-done.1
  31.4 0.6 %copy.13 = f32[4,128]{1,0:T(4,128)} copy(f32[4,128]{1,0:T(4,128)S(1)} %copy-done.1) | data formatting | bytes 4096
Async XLA Ops:
  29.4 1.3 %copy-start = (f32[32,128]{1,0:T(8,128)S(1)}, f32[32,128]{1,0:T(8,128)}, u32[]{:S(2)}) copy-start(f32[32,128]{1,0:T(8,128)} %get-tuple-element.7) | copy-start | bytes 49156
  30.7 0.7 %copy-start.1 = (f32[4,128]{1,0:T(4,128)S(1)}, f32[4,128]{1,0:T(4,128)}, u32[]{:S(2)}) copy-start(f32[4,128]{1,0:T(4,128)} %get-tuple-element.8) | copy-start | bytes 6148

commit v3 on v1

--- a/solution.py
+++ b/solution.py
@@ -12,6 +12,7 @@
 LEVELS = 4
 TILE = 128
 REPLICA_LIMIT = 16 * 2**20
+VMEM_LIMIT = 40 * 2**20
 
 
 def tile_products(source_rows, live_tiles, dest_slots, source_slots, row_tiles):
@@ -77,24 +78,14 @@
     return (hop_level, kept_weight * scale, counts)
 
 
-def near_order(depth):
-    table = []
-    for z in range(depth):
-        up = z < depth / 2
-        others = [other for other in range(depth) if other != z]
-        table.append(sorted(others, key=lambda o: (abs(o - z), (o < z) if up else (o > z))))
-    return table
-
-
-def pick(table, z, step):
-    value = jnp.int32(0)
-    for index, entries in enumerate(table):
-        value = jnp.where(z == index, jnp.int32(entries[step]), value)
-    return value
+def unpack(packed, hop_out, share_out, counts_out):
+    hop_out[...] = packed[pl.ds(0, PV)].astype(jnp.int32)
+    share_out[...] = packed[pl.ds(PV, PV)]
+    counts_out[...] = packed[pl.ds(2 * PV, LEVELS)]
 
 
 def kernel(
-    n_row, n_col, tiles_ref, pos_ref, total_ref, roots_ref, hop_out, share_out, counts_out,
+    n_row, n_col, tiles_ref, pos_ref, total_ref, roots_ref, packed,
     adj, front, hop, path, send_z, recv_z, send_n, recv_n, send_d, recv_d, send_s, recv_s, recv_sd,
 ):
     r = lax.axis_index("row")
@@ -108,10 +99,11 @@
     row_block, col_block = adj.shape[2], adj.shape[3]
     half = row_block // 2
     roots = roots_ref.shape[1]
-    table = near_order(depth)
+    steps = sorted(range(1, depth), key=lambda step: min(step, depth - step))
+    order = [z] + [(z + step) % depth for step in steps]
 
     barrier = pltpu.get_barrier_semaphore()
-    others = [(r, pick(table, z, step) * 2 + core) for step in range(depth - 1)]
+    others = [(r, zz * 2 + core) for zz in order[1:]]
     others += [(row_x, c), (row_y, c), (r, z * 2 + 1 - core)]
     for device in others:
         pl.semaphore_signal(barrier, inc=1, device_id=device, device_id_type=pl.DeviceIdType.MESH)
@@ -180,7 +172,6 @@
             arrive(piece(zz, row_d, axis), send_d.at[axis, zz], recv_d.at[axis, zz])
             send(piece(zz, row_d, axis), send_s.at[n_row + axis, zz], recv_sd.at[axis, zz], sibling)
 
-    order = [z] + [pick(table, z, step) for step in range(depth - 1)]
     spread(z)
     for step in range(depth - 1):
         zz = order[step + 1]
@@ -230,14 +221,14 @@
                 for cc in range(n_col):
                     front[later, pl.ds(cc * col_block + rr * PV, PV)] = narrow[cc * PV:(cc + 1) * PV]
         kept = kept + path[own]
-        counts_out[pl.ds(level, 1)] = count
+        packed[pl.ds(2 * PV + level, 1)] = count
         factors.append(count / jnp.maximum(total, 1.0))
     level_own = hop[own]
     scale = jnp.where(level_own == 0, 1.0, 0.0)
     for level in range(LEVELS):
         scale = jnp.where(level_own == level + 1, factors[level], scale)
-    hop_out[...] = level_own
-    share_out[...] = kept * scale
+    packed[pl.ds(0, PV)] = level_own.astype(jnp.float32)
+    packed[pl.ds(PV, PV)] = kept * scale
 
     for copy in started:
         copy.wait_send()
@@ -251,15 +242,11 @@
     vmem = pl.BlockSpec(memory_space=pltpu.VMEM)
     smem = pl.BlockSpec(memory_space=pltpu.SMEM)
     dma = pltpu.SemaphoreType.DMA
-    return pl.pallas_call(
+    packed = pl.pallas_call(
         functools.partial(kernel, n_row, n_col),
-        out_shape=(
-            jax.ShapeDtypeStruct((PV, roots), jnp.int32),
-            jax.ShapeDtypeStruct((PV, roots), jnp.float32),
-            jax.ShapeDtypeStruct((LEVELS, roots), jnp.float32),
-        ),
+        out_shape=jax.ShapeDtypeStruct((2 * PV + LEVELS, roots), jnp.float32),
         in_specs=[vmem, smem, smem, vmem],
-        out_specs=(vmem, vmem, vmem),
+        out_specs=vmem,
         scratch_shapes=[
             pltpu.VMEM((n_col, n_row, row_block, col_block), jnp.bfloat16),
             pltpu.VMEM((2, vertices, roots), jnp.bfloat16),
@@ -270,8 +257,19 @@
             dma((2, depth)), dma((2, depth)),
             dma((n_row + 2, depth)), dma((n_row, depth)), dma((2, depth)),
         ],
-        compiler_params=pltpu.CompilerParams(collective_id=0, has_side_effects=True),
+        compiler_params=pltpu.CompilerParams(collective_id=0, has_side_effects=True, vmem_limit_bytes=VMEM_LIMIT),
     )(tile_weights[0, 0], tile_pos[0, 0], tile_total, root_ids.reshape(1, roots))
+    return pl.pallas_call(
+        unpack,
+        out_shape=(
+            jax.ShapeDtypeStruct((PV, roots), jnp.int32),
+            jax.ShapeDtypeStruct((PV, roots), jnp.float32),
+            jax.ShapeDtypeStruct((LEVELS, roots), jnp.float32),
+        ),
+        in_specs=[vmem],
+        out_specs=(vmem, vmem, vmem),
+        compiler_params=pltpu.CompilerParams(vmem_limit_bytes=2**20),
+    )(packed)
 
 
 def solution(mesh):

time: 30 us -> 28.5 us (0.950)
  local copies, waits for them, and re-layouts: 2.58 us -> 1.51 us
  Pallas kernels: 25.8 us -> 25.5 us
    unnamed x7 -> x6, local copies, waits for them, and re-layouts: 2.58 us -> 1.51 us
    pallas_call x1 -> x2, Pallas kernels: 25.8 us -> 25.5 us  [the longest x1 24.9 us: replicated(): pl.pallas_call(functools.partial(kernel, n_row, n_col), out_shape=jax.Sha...]
where the time goes in v3:
time: 28.5 us; the launch traced here: 28.3 us
  Pallas kernels  25.5 us (89%)
  local copies, waits for them, and re-layouts  1.51 us (5%)
  between operations  1.3 us (5%)
    pallas_call x1, Pallas kernels, replicated(): pl.pallas_call(functools.partial(kernel, n_row, n_col), out_shape=jax.Sha...  24.9 us
    unnamed x6, local copies, waits for them, and re-layouts  1.51 us
    pallas_call x1, Pallas kernels, replicated(): pl.pallas_call(unpack, out_shape=(jax.ShapeDtypeStruct((PV, roots), jnp.i...  0.62 us

profile of v3, /device:TPU:1, one launch (start us, length us, event | category | flops | bytes accessed | tf_op | source)
XLA Modules:
  0.0 28.3 jit_solution(2860210188920182966)
XLA Ops:
  1.3 0.0 copy-start.1
  1.3 0.0 copy-start.2
  1.3 0.7 %copy-done.1 = s32[1,1,2,2]{3,2,1,0:T(2,128)S(1)} copy-done((s32[1,1,2,2]{3,2,1,0:T(2,128)S(1)}, s32[1,1,2,2]{3,2,1,0:T(2,128)}, u32[]{:S(2)}) %copy-start.1) | copy-done | bytes 40
  2.0 0.0 copy-done.2
  2.0 0.0 copy-start
  2.0 0.8 %copy-done = bf16[1,1,2,128,128]{4,3,2,1,0:T(8,128)(2,1)S(1)} copy-done((bf16[1,1,2,128,128]{4,3,2,1,0:T(8,128)(2,1)S(1)}, bf16[1,1,2,128,128]{4,3,2,1,0:T(8,128)(2,1)}, u32[]{:S(2)}) %copy-start) | copy-done | bytes 65560
  2.8 24.9 %shard_map.67.packed = f32[68,128]{1,0:T(8,128)S(1)} custom-call(bf16[2,128,128]{2,1,0:T(8,128)(2,1)S(1)} %bitcast.3, s32[2,2]{1,0:T(2,128)S(1)} %bitcast.4, s32[1,1]{1,0:T(1,128)S(6)} %copy.7.total_ref, s32[1,128]{1,0:T(1,128)S(1)} %bitcast.5), custom_call_target="tpu_custom_call" | custom-call | tf_op jit(solution)/shard_map/pallas_call | solution.py:245
  27.7 0.6 %shard_map.68 = (s32[32,128]{1,0:T(8,128)}, f32[32,128]{1,0:T(8,128)}, f32[4,128]{1,0:T(4,128)}) custom-call(f32[68,128]{1,0:T(8,128)S(1)} %shard_map.67.packed), custom_call_target="tpu_custom_call" | custom-call | tf_op jit(solution)/shard_map/pallas_call | solution.py:262
Async XLA Ops:
  1.3 0.7 %copy-start.1 = (s32[1,1,2,2]{3,2,1,0:T(2,128)S(1)}, s32[1,1,2,2]{3,2,1,0:T(2,128)}, u32[]{:S(2)}) copy-start(s32[1,1,2,2]{3,2,1,0:T(2,128)} %param.5) | copy-start | bytes 52
  1.3 0.7 %copy-start.2 = (s32[128]{0:T(128)S(1)}, s32[128]{0:T(128)}, u32[]{:S(2)}) copy-start(s32[128]{0:T(128)} %param.7) | copy-start | bytes 1540
  2.0 0.8 %copy-start = (bf16[1,1,2,128,128]{4,3,2,1,0:T(8,128)(2,1)S(1)}, bf16[1,1,2,128,128]{4,3,2,1,0:T(8,128)(2,1)}, u32[]{:S(2)}) copy-start(bf16[1,1,2,128,128]{4,3,2,1,0:T(8,128)(2,1)} %param.4) | copy-start | bytes 196612

commit v4 on v3

--- a/solution.py
+++ b/solution.py
@@ -85,9 +85,17 @@
 
 
 def kernel(
-    n_row, n_col, tiles_ref, pos_ref, total_ref, roots_ref, packed,
-    adj, front, hop, path, send_z, recv_z, send_n, recv_n, send_d, recv_d, send_s, recv_s, recv_sd,
+    n_row, n_col, tiles_hbm, pos_hbm, total_hbm, roots_hbm, packed,
+    tiles_ref, pos_ref, total_ref, roots_ref, load_sem, adj, front, hop, path, send_z, recv_z, send_n, recv_n, send_d, recv_d, send_s, recv_s, recv_sd,
 ):
+    loads = [
+        pltpu.make_async_copy(source, target, load_sem.at[index])
+        for index, (source, target) in enumerate(
+            ((tiles_hbm, tiles_ref), (pos_hbm, pos_ref), (total_hbm, total_ref), (roots_hbm, roots_ref))
+        )
+    ]
+    for load in loads:
+        load.start()
     r = lax.axis_index("row")
     c = lax.axis_index("col")
     z, core = c // 2, c % 2
@@ -108,6 +116,8 @@
     for device in others:
         pl.semaphore_signal(barrier, inc=1, device_id=device, device_id_type=pl.DeviceIdType.MESH)
 
+    for load in loads:
+        load.wait()
     for tr in range(row_block // TILE):
         for tc in range(col_block // TILE):
             value = jnp.zeros((TILE, TILE), jnp.float32)
@@ -116,6 +126,59 @@
                 value = value + tiles_ref[s].astype(jnp.float32) * here.astype(jnp.float32)
             adj[c, r, pl.ds(tr * TILE, TILE), pl.ds(tc * TILE, TILE)] = value.astype(jnp.bfloat16)
 
+    pl.semaphore_wait(barrier, len(others))
+
+    started = []
+
+    def send(ref, send_sem, recv_sem, device):
+        copy = pltpu.make_async_remote_copy(
+            src_ref=ref, dst_ref=ref, send_sem=send_sem, recv_sem=recv_sem,
+            device_id=device, device_id_type=pl.DeviceIdType.MESH,
+        )
+        copy.start()
+        started.append(copy)
+
+    def arrive(ref, send_sem, recv_sem):
+        pltpu.make_async_remote_copy(
+            src_ref=ref, dst_ref=ref, send_sem=send_sem, recv_sem=recv_sem,
+            device_id=(r, z * 2 + 1 - core), device_id_type=pl.DeviceIdType.MESH,
+        ).wait_recv()
+
+    def block(zz, rr):
+        return adj.at[zz * 2 + core, rr]
+
+    def piece(zz, rr, h):
+        return adj.at[zz * 2 + core, rr, pl.ds(h * half, half)]
+
+    sibling = (r, z * 2 + 1 - core)
+
+    def spread(zz):
+        for turn in range(2):
+            for axis in range(2):
+                h = axis if turn == 0 else 1 - axis
+                send(piece(zz, r, h), send_n.at[axis, h, zz], recv_n.at[axis, h, zz], (rows[axis], c))
+
+    def share_block(zz, rr):
+        send(block(zz, rr), send_s.at[rr, zz], recv_s.at[rr, zz], sibling)
+
+    def relay(zz):
+        for axis in range(2):
+            arrive(piece(zz, rows[axis], axis), send_n.at[axis, axis, zz], recv_n.at[axis, axis, zz])
+            send(piece(zz, rows[axis], axis), send_d.at[axis, zz], recv_d.at[axis, zz], (rows[1 - axis], c))
+        for axis in range(2):
+            arrive(piece(zz, rows[axis], 1 - axis), send_n.at[axis, 1 - axis, zz], recv_n.at[axis, 1 - axis, zz])
+            share_block(zz, rows[axis])
+
+    def finish(zz):
+        for axis in range(2):
+            arrive(piece(zz, row_d, axis), send_d.at[axis, zz], recv_d.at[axis, zz])
+            send(piece(zz, row_d, axis), send_s.at[n_row + axis, zz], recv_sd.at[axis, zz], sibling)
+
+    spread(z)
+    for step in range(depth - 1):
+        zz = order[step + 1]
+        send(block(z, r), send_z.at[zz], recv_z.at[z], (r, zz * 2 + core))
+    share_block(z, r)
     for rr in range(n_row):
         part = pl.ds(rr * row_block, row_block)
         ids = rr * row_block + lax.broadcasted_iota(jnp.int32, (row_block, roots), 0)
@@ -126,57 +189,6 @@
             front[0, pl.ds(cc * col_block + rr * PV, PV)] = (
                 is_root[cc * PV:(cc + 1) * PV].astype(jnp.float32).astype(jnp.bfloat16)
             )
-
-    pl.semaphore_wait(barrier, len(others))
-
-    started = []
-
-    def send(ref, send_sem, recv_sem, device):
-        copy = pltpu.make_async_remote_copy(
-            src_ref=ref, dst_ref=ref, send_sem=send_sem, recv_sem=recv_sem,
-            device_id=device, device_id_type=pl.DeviceIdType.MESH,
-        )
-        copy.start()
-        started.append(copy)
-
-    def arrive(ref, send_sem, recv_sem):
-        pltpu.make_async_remote_copy(
-            src_ref=ref, dst_ref=ref, send_sem=send_sem, recv_sem=recv_sem,
-            device_id=(r, z * 2 + 1 - core), device_id_type=pl.DeviceIdType.MESH,
-        ).wait_recv()
-
-    def block(zz, rr):
-        return adj.at[zz * 2 + core, rr]
-
-    def piece(zz, rr, h):
-        return adj.at[zz * 2 + core, rr, pl.ds(h * half, half)]
-
-    sibling = (r, z * 2 + 1 - core)
-
-    def spread(zz):
-        for axis in range(2):
-            send(block(zz, r), send_n.at[axis, zz], recv_n.at[axis, zz], (rows[axis], c))
-
-    def share_block(zz, rr):
-        send(block(zz, rr), send_s.at[rr, zz], recv_s.at[rr, zz], sibling)
-
-    def relay(zz):
-        for axis in range(2):
-            arrive(block(zz, rows[axis]), send_n.at[axis, zz], recv_n.at[axis, zz])
-            send(piece(zz, rows[axis], axis), send_d.at[axis, zz], recv_d.at[axis, zz], (rows[1 - axis], c))
-        for axis in range(2):
-            share_block(zz, rows[axis])
-
-    def finish(zz):
-        for axis in range(2):
-            arrive(piece(zz, row_d, axis), send_d.at[axis, zz], recv_d.at[axis, zz])
-            send(piece(zz, row_d, axis), send_s.at[n_row + axis, zz], recv_sd.at[axis, zz], sibling)
-
-    spread(z)
-    for step in range(depth - 1):
-        zz = order[step + 1]
-        send(block(z, r), send_z.at[zz], recv_z.at[z], (r, zz * 2 + core))
-    share_block(z, r)
     for step in range(depth):
         if step + 1 < depth:
             zz = order[step + 1]
@@ -240,20 +252,25 @@
     vertices = n_row * row_block
     depth = n_col // 2
     vmem = pl.BlockSpec(memory_space=pltpu.VMEM)
-    smem = pl.BlockSpec(memory_space=pltpu.SMEM)
+    hbm = pl.BlockSpec(memory_space=pltpu.HBM)
     dma = pltpu.SemaphoreType.DMA
     packed = pl.pallas_call(
         functools.partial(kernel, n_row, n_col),
         out_shape=jax.ShapeDtypeStruct((2 * PV + LEVELS, roots), jnp.float32),
-        in_specs=[vmem, smem, smem, vmem],
+        in_specs=[hbm, hbm, hbm, hbm],
         out_specs=vmem,
         scratch_shapes=[
+            pltpu.VMEM(tile_weights.shape[2:], tile_weights.dtype),
+            pltpu.SMEM(tile_pos.shape[2:], jnp.int32),
+            pltpu.SMEM(tile_total.shape, jnp.int32),
+            pltpu.VMEM((1, roots), jnp.int32),
+            dma((4,)),
             pltpu.VMEM((n_col, n_row, row_block, col_block), jnp.bfloat16),
             pltpu.VMEM((2, vertices, roots), jnp.bfloat16),
             pltpu.VMEM((vertices, roots), jnp.int32),
             pltpu.VMEM((vertices, roots), jnp.float32),
             dma((depth,)), dma((depth,)),
-            dma((2, depth)), dma((2, depth)),
+            dma((2, 2, depth)), dma((2, 2, depth)),
             dma((2, depth)), dma((2, depth)),
             dma((n_row + 2, depth)), dma((n_row, depth)), dma((2, depth)),
         ],

time: 28.5 us -> 27.9 us (0.979)
  Pallas kernels: 25.5 us -> 24.9 us
    pallas_call x1, Pallas kernels: 24.9 us -> 24.2 us  [replicated(): pl.pallas_call(functools.partial(kernel, n_row, n_col), out_shape=jax.Sha...]
where the time goes in v4:
time: 27.9 us; the launch traced here: 27.7 us
  Pallas kernels  24.9 us (89%)
  local copies, waits for them, and re-layouts  1.51 us (5%)
  between operations  1.3 us (5%)
    pallas_call x1, Pallas kernels, replicated(): pl.pallas_call(functools.partial(kernel, n_row, n_col), out_shape=jax.Sha...  24.2 us
    unnamed x6, local copies, waits for them, and re-layouts  1.51 us
    pallas_call x1, Pallas kernels, replicated(): pl.pallas_call(unpack, out_shape=(jax.ShapeDtypeStruct((PV, roots), jnp.i...  0.62 us

profile of v4, /device:TPU:1, one launch (start us, length us, event | category | flops | bytes accessed | tf_op | source)
XLA Modules:
  0.0 27.7 jit_solution(7310126930465407748)
XLA Ops:
  1.3 0.0 copy-start.1
  1.3 0.0 copy-start.2
  1.3 0.7 %copy-done.1 = s32[1,1,2,2]{3,2,1,0:T(2,128)S(1)} copy-done((s32[1,1,2,2]{3,2,1,0:T(2,128)S(1)}, s32[1,1,2,2]{3,2,1,0:T(2,128)}, u32[]{:S(2)}) %copy-start.1) | copy-done | bytes 40
  2.0 0.0 copy-done.2
  2.0 0.0 copy-start
  2.0 0.8 %copy-done = bf16[1,1,2,128,128]{4,3,2,1,0:T(8,128)(2,1)S(1)} copy-done((bf16[1,1,2,128,128]{4,3,2,1,0:T(8,128)(2,1)S(1)}, bf16[1,1,2,128,128]{4,3,2,1,0:T(8,128)(2,1)}, u32[]{:S(2)}) %copy-start) | copy-done | bytes 65560
  2.8 24.2 %shard_map.67.packed = f32[68,128]{1,0:T(8,128)S(1)} custom-call(bf16[2,128,128]{2,1,0:T(8,128)(2,1)S(1)} %bitcast.3, s32[2,2]{1,0:T(2,128)S(1)} %bitcast.4, s32[1,1]{1,0:T(1,128)S(6)} %copy.7.total_hbm, s32[1,128]{1,0:T(1,128)S(1)} %bitcast.5), custom_call_target="tpu_custom_call" | custom-call | tf_op jit(solution)/shard_map/pallas_call | solution.py:257
  27.1 0.6 %shard_map.68 = (s32[32,128]{1,0:T(8,128)}, f32[32,128]{1,0:T(8,128)}, f32[4,128]{1,0:T(4,128)}) custom-call(f32[68,128]{1,0:T(8,128)S(1)} %shard_map.67.packed), custom_call_target="tpu_custom_call" | custom-call | tf_op jit(solution)/shard_map/pallas_call | solution.py:279
Async XLA Ops:
  1.3 0.7 %copy-start.1 = (s32[1,1,2,2]{3,2,1,0:T(2,128)S(1)}, s32[1,1,2,2]{3,2,1,0:T(2,128)}, u32[]{:S(2)}) copy-start(s32[1,1,2,2]{3,2,1,0:T(2,128)} %param.5) | copy-start | bytes 52
  1.3 0.7 %copy-start.2 = (s32[128]{0:T(128)S(1)}, s32[128]{0:T(128)}, u32[]{:S(2)}) copy-start(s32[128]{0:T(128)} %param.7) | copy-start | bytes 1540
  2.0 0.8 %copy-start = (bf16[1,1,2,128,128]{4,3,2,1,0:T(8,128)(2,1)S(1)}, bf16[1,1,2,128,128]{4,3,2,1,0:T(8,128)(2,1)}, u32[]{:S(2)}) copy-start(bf16[1,1,2,128,128]{4,3,2,1,0:T(8,128)(2,1)} %param.4) | copy-start | bytes 196612
